TPU v7x, 128 devices: a whole 4x4x4 slice. The times are simulated.
128 devices in a mesh: section: 4 (over y), dp: 32 (over x, z, core).
Axes of the slice: x: 4, y: 4, z: 4, core: 2. Of those that a mesh axis runs over, the one named last changes fastest.
Arguments:
- inputs: bfloat16 [4096, 1600], P('dp'), may hold values from -6 to 6
- targets: bfloat16 [4096, 1600], P('dp'), may hold values from -6 to 6
- weight_in: bfloat16 [4, 1600, 3200], P('section'), may hold values from -0.15625 to 0.15625
- hidden_bias: float32 [4, 3200], P('section'), may hold values from -3 to 3
- norm_gain: float32 [4, 1600], P('section'), may hold values from 0.5 to 1.5
- weight_out: bfloat16 [4, 3200, 1600], P('section'), may hold values from -0.109375 to 0.109375
- current: float32 [4, 3200, 1600], P('section', 'dp')
- previous: float32 [4, 3200, 1600], P('section', 'dp')
- older_basis: float32 [2, 4, 3200, 1600], P(None, 'section', 'dp')
- beta_before: float32 [1], replicated, may hold values from 1 to 4
Outputs:
- next_vector: float32 [4, 3200, 1600], P('section', 'dp')
- tridiagonal_entries: float32 [2], replicated
All inputs are finite; a program needn't handle non-finite values.
Results may differ from a plain program's by a relative error of at most 0.012.
Values may be sent and summed in bfloat16 or wider, within the bound.
A program may use at most 192 MiB of HBM per device.

v0:
```python
from functools import partial
import functools
import jax
import jax.numpy as jnp
from jax import lax
from jax.sharding import Mesh
from jax.sharding import PartitionSpec as P

DP = ("dp_0", "dp_1", "dp_2")
SECTION_DP = ("section", "dp_0", "dp_1", "dp_2")


def laid_out(blocks, dim):
    dims = list(blocks.shape[1:])
    dims[dim] *= blocks.shape[0]
    return jnp.moveaxis(blocks, 0, dim).reshape(dims)


def gather_in_order(value, axes, turns):
    blocks = value[None]
    for k in turns:
        blocks = lax.all_gather(blocks, axes[k], axis=0, tiled=True)
    carried = [lax.axis_size(axes[k]) for k in reversed(turns)]
    blocks = blocks.reshape(*carried, *value.shape)
    turned = sorted(range(len(turns)), key=lambda place: turns[len(turns) - 1 - place])
    return blocks.transpose(*turned, *range(len(turns), blocks.ndim)).reshape(-1, *value.shape)


def gathered_by_axis(value, axes, turns, dim):
    return laid_out(gather_in_order(value, axes, turns), dim)


def from_behind(value, axis, steps):
    count = lax.axis_size(axis)
    initial, last = (max(0, -steps), min(count, count - steps))
    return lax.ppermute(value, axis, [(source, source + steps) for source in range(initial, last)])


def sent_together(arrays, axis, dim, along):
    ends, at = ([], 0)
    for a in arrays[:-1]:
        at += a.shape[along]
        ends.append(at)
    both = jnp.concatenate(arrays, axis=along)
    return tuple(jnp.split(lax.all_gather(both, axis, axis=dim, tiled=True), ends, axis=along))


def over_axes(value, axes):
    return functools.reduce(lax.psum, axes, value)


def gelu_tanh(values):
    return jax.nn.gelu(values, approximate=True)


def gelu_slope(values):
    return jax.jvp(gelu_tanh, (values,), (jnp.ones_like(values),))[1]


def gelu_bend(values):
    return jax.jvp(gelu_slope, (values,), (jnp.ones_like(values),))[1]


def normalize(values, gain_row):
    mean_value = jnp.mean(values, axis=-1, keepdims=True)
    centered = values - mean_value
    variance = jnp.mean(centered * centered, axis=-1, keepdims=True)
    return centered * lax.rsqrt(variance + 1e-05) * gain_row


def times_transposed(left, right):
    return lax.dot_general(
        left, right, (((1,), (1,)), ((), ())), preferred_element_type=jnp.float32
    )


def pick_block(stack, position):
    return lax.dynamic_index_in_dim(stack, position, 0, keepdims=False)


def store_block(stack, block, position, active):
    return jnp.where(active, lax.dynamic_update_index_in_dim(stack, block, position, 0), stack)


def body(
    inputs,
    targets,
    weight_in,
    hidden_bias,
    norm_gain,
    weight_out,
    current,
    previous,
    older_basis,
    beta_before,
):
    section_index = lax.axis_index("section")
    sections = lax.axis_size("section")
    replicas = lax.axis_size(DP)
    layer_in = weight_in[0]
    bias_row = hidden_bias[0]
    gain_row = norm_gain[0]
    layer_out = weight_out[0]
    direction = gathered_by_axis(
        current[0].astype(jnp.bfloat16), (("dp_0", "dp_1"), "dp_2"), (0, 1), 0
    )
    pieces = 2
    local_rows, width = inputs.shape
    hidden_width = layer_in.shape[1]
    block_rows = local_rows // pieces
    row_count = float(local_rows * replicas)
    blocks_in = inputs.reshape(pieces, block_rows, width)
    blocks_goal = targets.reshape(pieces, block_rows, width)
    empty_rows = jnp.zeros((block_rows, width), jnp.bfloat16)
    empty_hidden = jnp.zeros((block_rows, hidden_width), jnp.bfloat16)
    empty_pre = jnp.zeros((block_rows, hidden_width), jnp.float32)
    empty_stack = jnp.zeros((pieces, block_rows, width), jnp.bfloat16)
    hidden_stack = jnp.zeros((pieces, block_rows, hidden_width), jnp.bfloat16)
    pre_stack = jnp.zeros((pieces, block_rows, hidden_width), jnp.float32)
    kept_rows, kept_tangent = (empty_stack, empty_stack)
    final_rows, final_tangent = (empty_stack, empty_stack)
    hidden_dot_stack = hidden_stack
    preact_stack, preact_dot_stack = (pre_stack, pre_stack)
    arrived_rows, arrived_tangent = (empty_rows, empty_rows)
    tick_count = pieces + sections - 1

    def run_layer(operands):
        rows_float = operands[0].astype(jnp.float32)
        tangent_float = operands[1].astype(jnp.float32)
        normed, normed_dot = jax.jvp(
            partial(normalize, gain_row=gain_row), (rows_float,), (tangent_float,)
        )
        stacked_norm = jnp.concatenate(
            [normed.astype(jnp.bfloat16), normed_dot.astype(jnp.bfloat16)], axis=0
        )
        pre_both = jnp.dot(stacked_norm, layer_in, preferred_element_type=jnp.float32)
        preact = pre_both[:block_rows] + bias_row
        preact_dot = pre_both[block_rows:]
        hidden = gelu_tanh(preact).astype(jnp.bfloat16)
        hidden_dot = (gelu_slope(preact) * preact_dot).astype(jnp.bfloat16)
        out_both = jnp.dot(
            jnp.concatenate([hidden, hidden_dot], axis=0),
            layer_out,
            preferred_element_type=jnp.float32,
        )
        rows_out = rows_float + out_both[:block_rows]
        tangent_out = tangent_float + out_both[block_rows:]
        tangent_out = tangent_out + jnp.dot(hidden, direction, preferred_element_type=jnp.float32)
        return (
            rows_out.astype(jnp.bfloat16),
            tangent_out.astype(jnp.bfloat16),
            preact,
            preact_dot,
            hidden,
            hidden_dot,
        )

    def skip_layer(operands):
        return (empty_rows, empty_rows, empty_pre, empty_pre, empty_hidden, empty_hidden)

    for step_number in range(tick_count):
        micro_slot = step_number - section_index
        active = jnp.logical_and(micro_slot >= 0, micro_slot < pieces)
        position = jnp.clip(micro_slot, 0, pieces - 1)
        feed_rows = jnp.where(section_index == 0, pick_block(blocks_in, position), arrived_rows)
        feed_tangent = jnp.where(section_index == 0, empty_rows, arrived_tangent)
        out_rows, out_tangent, preact, preact_dot, hidden, hidden_dot = lax.cond(
            active, run_layer, skip_layer, (feed_rows, feed_tangent)
        )
        kept_rows = store_block(kept_rows, feed_rows, position, active)
        kept_tangent = store_block(kept_tangent, feed_tangent, position, active)
        final_rows = store_block(final_rows, out_rows, position, active)
        final_tangent = store_block(final_tangent, out_tangent, position, active)
        preact_stack = store_block(preact_stack, preact, position, active)
        preact_dot_stack = store_block(preact_dot_stack, preact_dot, position, active)
        hidden_stack = store_block(hidden_stack, hidden, position, active)
        hidden_dot_stack = store_block(hidden_dot_stack, hidden_dot, position, active)
        if step_number + 1 < tick_count:
            arrived_rows, arrived_tangent = from_behind((out_rows, out_tangent), "section", 1)

    def run_back(operands):
        rows_float = operands[0].astype(jnp.float32)
        tangent_float = operands[1].astype(jnp.float32)
        preact, preact_dot, grad_out, grad_dot_out = (
            operands[2],
            operands[3],
            operands[4],
            operands[5],
        )
        back_both = times_transposed(jnp.concatenate([grad_out, grad_dot_out], axis=0), layer_out)
        back_hidden = back_both[:block_rows]
        back_hidden_dot = back_both[block_rows:] + times_transposed(grad_out, direction)
        slope = gelu_slope(preact)
        pre_grad = (slope * back_hidden).astype(jnp.bfloat16)
        pre_grad_dot = (
            gelu_bend(preact) * preact_dot * back_hidden + slope * back_hidden_dot
        ).astype(jnp.bfloat16)
        norm_both = times_transposed(jnp.concatenate([pre_grad, pre_grad_dot], axis=0), layer_in)
        norm_grad = norm_both[:block_rows]
        norm_grad_dot = norm_both[block_rows:]

        def pull_back(values, cotangent):
            return jax.vjp(partial(normalize, gain_row=gain_row), values)[1](cotangent)[0]

        grad_in, grad_in_dot = jax.jvp(
            pull_back, (rows_float, norm_grad), (tangent_float, norm_grad_dot)
        )
        grad_next = (grad_out.astype(jnp.float32) + grad_in).astype(jnp.bfloat16)
        grad_dot_next = (grad_dot_out.astype(jnp.float32) + grad_in_dot).astype(jnp.bfloat16)
        return (grad_next, grad_dot_next)

    def skip_back(operands):
        return (empty_rows, empty_rows)

    grad_stack, grad_dot_stack = (empty_stack, empty_stack)
    arrived_grad, arrived_grad_dot = (empty_rows, empty_rows)
    last_section = sections - 1
    for step_number in range(tick_count):
        micro_slot = step_number - (last_section - section_index)
        active = jnp.logical_and(micro_slot >= 0, micro_slot < pieces)
        position = jnp.clip(micro_slot, 0, pieces - 1)
        top_rows = pick_block(final_rows, position).astype(jnp.float32)
        top_tangent = pick_block(final_tangent, position).astype(jnp.float32)
        goal_rows = pick_block(blocks_goal, position).astype(jnp.float32)
        own_grad = ((top_rows - goal_rows) / row_count).astype(jnp.bfloat16)
        own_grad_dot = (top_tangent / row_count).astype(jnp.bfloat16)
        feed_grad = jnp.where(section_index == last_section, own_grad, arrived_grad)
        feed_grad_dot = jnp.where(section_index == last_section, own_grad_dot, arrived_grad_dot)
        operands = (
            pick_block(kept_rows, position),
            pick_block(kept_tangent, position),
            pick_block(preact_stack, position),
            pick_block(preact_dot_stack, position),
            feed_grad,
            feed_grad_dot,
        )
        grad_next, grad_dot_next = lax.cond(active, run_back, skip_back, operands)
        grad_stack = store_block(grad_stack, feed_grad, position, active)
        grad_dot_stack = store_block(grad_dot_stack, feed_grad_dot, position, active)
        if step_number + 1 < tick_count:
            arrived_grad, arrived_grad_dot = from_behind((grad_next, grad_dot_next), "section", -1)
    hidden_rows = hidden_stack.reshape(local_rows, hidden_width)
    hidden_dot_rows = hidden_dot_stack.reshape(local_rows, hidden_width)
    grad_rows = grad_stack.reshape(local_rows, width)
    grad_dot_rows = grad_dot_stack.reshape(local_rows, width)
    hidden_share, slope_share = (
        lax.all_to_all(hidden_rows.T, DP, split_axis=0, concat_axis=1, tiled=True),
        lax.all_to_all(hidden_dot_rows.T, DP, split_axis=0, concat_axis=1, tiled=True),
    )
    gathered = sent_together((grad_rows, grad_dot_rows), DP, 0, 1)
    running = jnp.dot(slope_share, gathered[0], preferred_element_type=jnp.float32)
    hvp = (running + jnp.dot(hidden_share, gathered[1], preferred_element_type=jnp.float32))[None]
    entry_count = float(hvp.size * sections * replicas)
    basis = jnp.concatenate([older_basis, previous[None], current[None]], axis=0)
    members = basis.shape[0]
    stacked = jnp.concatenate([basis, hvp[None]], axis=0).reshape(members + 1, -1)
    local_gram = lax.dot_general(
        stacked,
        stacked,
        (((1,), (1,)), ((), ())),
        precision=lax.Precision.HIGHEST,
        preferred_element_type=jnp.float32,
    )
    gram = over_axes(local_gram, SECTION_DP) / entry_count
    basis_gram = gram[:members, :members]
    cross = gram[:members, members]
    square_hvp = gram[members, members]
    indices = jnp.arange(members)
    weights_start = jnp.where(indices == members - 2, -beta_before[0], 0.0)
    alpha_value = cross[members - 1] + jnp.sum(weights_start * basis_gram[:, members - 1])
    weights_first = weights_start - jnp.where(indices == members - 1, alpha_value, 0.0)
    coeffs = cross + jnp.sum(basis_gram * weights_first[:, None], axis=0)
    weights_second = weights_first - coeffs
    quadratic = jnp.sum(weights_second[:, None] * basis_gram * weights_second[None, :])
    square_second = square_hvp + 2.0 * jnp.sum(weights_second * cross) + quadratic
    beta_value = jnp.sqrt(jnp.maximum(square_second, 0.0) + 1e-06)
    second = hvp + jnp.sum(weights_second[:, None, None, None] * basis, axis=0)
    return (second / beta_value, jnp.stack([alpha_value, beta_value]))


def solution(mesh):
    finer = Mesh(
        mesh.devices.reshape(mesh.shape["section"], 4, 4, 2), ("section", "dp_0", "dp_1", "dp_2")
    )
    in_specs = (
        P(DP, None),
        P(DP, None),
        P("section", None, None),
        P("section", None),
        P("section", None),
        P("section", None, None),
        P("section", DP, None),
        P("section", DP, None),
        P(None, "section", DP, None),
        P(),
    )
    out_specs = (P("section", DP, None), P())
    return jax.shard_map(body, mesh=finer, in_specs=in_specs, out_specs=out_specs, check_vma=False)
```

profile of v0, /device:TPU:1, one launch (start us, length us, event | category | flops | bytes accessed | tf_op | source)
XLA Modules:
  0.0 732.1 jit_solution(5869003339484082788)
XLA Ops:
  9.1 62.4 %all-gather.4.cloned.1.call-done = bf16[16,100,1600]{2,1,0:T(8,128)(2,1)} async-done(((bf16[1,100,1600]{2,1,0:T(8,128)(2,1)}), bf16[16,100,1600]{2,1,0:T(8,128)(2,1)}) %all-gather.4.cloned.1.call-update) | async-done | bytes 5120016 | tf_op jit(solution)/shard_map/all_gather | solution.py:22
  71.5 5.6 copy.180
  79.4 16.9 %copy.178 = bf16[1,3200,1600]{2,1,0:T(8,128)(2,1)} copy(bf16[1,3200,1600]{1,2,0:T(8,128)(2,1)} %param.33) | data formatting | bytes 20480000 | tf_op args[5]
  96.5 6.5 all-gather.6.cloned.1.call-done
  103.0 10.0 %copy.280 = bf16[2,16,100,1600]{3,2,0,1:T(8,128)(2,1)} copy(bf16[2,16,100,1600]{3,1,0,2:T(8,128)(2,1)} %bitcast.647) | data formatting | bytes 20480000 | tf_op jit(solution)/shard_map/reshape | solution.py:24
  113.0 14.7 %reshape_reshape.3 = bf16[3200,1600]{1,0:T(8,128)(2,1)} reshape(bf16[16,2,100,1600]{3,2,1,0:T(8,128)(2,1)} %bitcast.644) | data formatting | bytes 20480000 | tf_op jit(solution)/shard_map/reshape;reshape | solution.py:16
  127.8 25.5 %conditional.9 = (f32[64,3200]{1,0:T(8,128)}, f32[64,3200]{1,0:T(8,128)S(1)}, bf16[1,64,3200]{2,1,0:T(8,128)(2,1)S(1)}, bf16[1,64,3200]{2,1,0:T(8,128)(2,1)}, bf...) conditional(s32[]{:T(128)} %convert_element_type.470, () %tuple.151, (bf16[1,64,1600]{2,1,0:T(8,128)(2,1)S(1)}, ...), branch_computations={%region_0.1_spmd, %region_1.5_spmd} | conditional | flops 3289190656 | bytes 78807200 | solution.py:167
  129.6 5.9 fusion.29
  142.7 8.2 %fusion = bf16[64,1600]{0,1:T(8,128)(2,1)S(1)} fusion(bf16[64,3200]{1,0:T(8,128)(2,1)S(1)} %multiply_convert_fusion, bf16[3200,1600]{1,0:T(8,128)(2,1)} %get-tuple-element.500, f32[128,1600]{0,1:T(8,128)S(1)} %fusion.25), kind=kOutput, calls=%fused_computation.1 | convolution fusion | flops 655564800 | bytes 11264000 | tf_op jit(solution)/shard_map/cond/branch_1_fun/dot_general | solution.py:148
  164.0 34.1 %conditional.10 = (bf16[64,1600]{0,1:T(8,128)(2,1)}, bf16[64,1600]{0,1:T(8,128)(2,1)}, f32[1,64,3200]{2,1,0:T(8,128)}, f32[1,64,3200]{2,1,0:T(8,128)}, bf16[1,64...) conditional(s32[]{:T(128)} %convert_element_type.472, ...), branch_computations={%region_5.6_spmd, %region_6.11_spmd} | conditional | flops 3286835456 | bytes 77476808 | solution.py:167
  171.5 5.9 fusion.68
  179.4 5.4 fusion.63
  184.9 9.1 %fusion.36 = bf16[64,1600]{0,1:T(8,128)(2,1)} fusion(bf16[64,3200]{1,0:T(8,128)(2,1)} %get-tuple-element.1010, bf16[3200,1600]{1,0:T(8,128)(2,1)} %get-tuple-element.507, bf16[64,1600]{0,1:T(8,128)(2,1)S(1)} %copy-done.21, f32[128,1600]{0,1:T(8,128)S(1)} %fusion.63), kind=kOutput, calls=%fused_computation.50 | convolution fusion | flops 655769600 | bytes 11468800 | tf_op jit(solution)/shard_map/cond/branch_1_fun/dot_general | solution.py:148
  214.7 5.5 conditional.11
  224.0 34.1 %collective-permute-start.5 = (bf16[64,1600]{1,0:T(8,128)(2,1)}, bf16[64,1600]{1,0:T(8,128)(2,1)S(1)}, u32[]{:S(2)}, u32[]{:S(2)}) collective-permute-start(bf16[64,1600]{1,0:T(8,128)(2,1)} %copy.193), channel_id=1, source_target_pairs={{0,32},{32,64},{64,96},{1,33},{33,65},{65,97},{2,34},{34,66},{66,9... | collective-permute-start | bytes 614408 | tf_op jit(solution)/shard_map/ppermute | solution.py:36
  279.8 32.4 %collective-permute-start.6 = (bf16[64,1600]{1,0:T(8,128)(2,1)}, bf16[64,1600]{1,0:T(8,128)(2,1)S(1)}, u32[]{:S(2)}, u32[]{:S(2)}) collective-permute-start(bf16[64,1600]{1,0:T(8,128)(2,1)} %copy.196), channel_id=1, source_target_pairs={{0,32},{32,64},{64,96},{1,33},{33,65},{65,97},{2,34},{34,66},{66,9... | collective-permute-start | bytes 614408 | tf_op jit(solution)/shard_map/ppermute | solution.py:36
  365.5 120.2 %collective-permute-done.13 = bf16[64,1600]{1,0:T(8,128)(2,1)S(1)} collective-permute-done((bf16[64,1600]{1,0:T(8,128)(2,1)S(1)}, bf16[64,1600]{1,0:T(8,128)(2,1)S(1)}, u32[]{:S(2)}, u32[]{:S(2)}) %collective-permute-start.13) | collective-permute-done | bytes 204832 | tf_op jit(solution)/shard_map/ppermute | solution.py:36
  493.2 27.1 %conditional.17 = (bf16[64,1600]{0,1:T(8,128)(2,1)}, bf16[64,1600]{0,1:T(8,128)(2,1)}) conditional(s32[]{:T(128)} %convert_element_type.508, () %tuple.167, (bf16[64,1600]{1,0:T(8,128)(2,1)S(1)}, f32[2,64,3200]{2,1,0:T(8,128)S(1)}, s32[]{:T(128)}, bf16[64,1600]{1,0:T(8,128)(2,1)S(1)}, bf16[3200,1600]{1,0:T(8,128)(2,1)}, ...), branch_computations={%region_59.60_spmd, %region_60.69_spmd} | conditional | flops 3295233024 | bytes 87697088 | solution.py:237
  495.6 7.7 %fusion.369 = f32[128,3200]{1,0:T(8,128)S(1)} fusion(bf16[3200,1600]{1,0:T(8,128)(2,1)} %get-tuple-element.568, bf16[64,1600]{0,1:T(8,128)(2,1)S(1)} %copy.234, bf16[64,1600]{0,1:T(8,128)(2,1)} %copy.233), kind=kOutput, calls=%fused_computation.554 | convolution fusion | flops 1311539200 | bytes 12288000 | tf_op jit(solution)/shard_map/cond/branch_1_fun/dot_general | solution.py:72
  503.4 7.4 %fusion.334 = bf16[64,3200]{1,0:T(8,128)(2,1)S(1)} fusion(bf16[64,1600]{1,0:T(8,128)(2,1)S(1)} %get-tuple-element.905, bf16[3200,1600]{1,0:T(8,128)(2,1)} %get-tuple-element.570, f32[128,3200]{1,0:T(8,128)S(1)} %fusion.369, f32[2,64,3200]{2,1,0:T(8,128)S(1)} %copy-done.6, s32[]{:T(128)} %get-tuple-element.566, f32[2,64,3200]{2,1,0:T(8,128)S(1)} %get-tuple-element.565), kind=kOutput, calls=%fused_computation.501 | convolution fusion | flops 661913600 | bytes 14131204 | tf_op jit(solution)/shard_map/cond/branch_1_fun/dot_general | solution.py:72
  542.5 9.8 %all-to-all-start = ((bf16[32,100,128]{2,1,0:T(8,128)(2,1)}), bf16[32,100,128]{2,1,0:T(8,128)(2,1)}, u32[]{:S(2)}, u32[]{:S(2)}) async-start(bf16[32,100,128]{2,1,0:T(8,128)(2,1)} %all_to_all.28), calls=%async_computation | async-start | bytes 1703936 | tf_op jit(solution)/shard_map/all_to_all | solution.py:248
  554.4 20.7 %all-to-all-done = bf16[32,100,128]{2,1,0:T(8,128)(2,1)} async-done(((bf16[32,100,128]{2,1,0:T(8,128)(2,1)}), bf16[32,100,128]{2,1,0:T(8,128)(2,1)}, u32[]{:S(2)}, u32[]{:S(2)}) %all-to-all-start) | async-done | bytes 819232 | tf_op jit(solution)/shard_map/all_to_all | solution.py:248
  575.1 5.5 all-to-all-start.1
  585.7 12.4 %all-to-all-done.1 = bf16[32,100,128]{2,1,0:T(8,128)(2,1)S(1)} async-done(((bf16[32,100,128]{2,1,0:T(8,128)(2,1)}), bf16[32,100,128]{2,1,0:T(8,128)(2,1)S(1)}, u32[]{:S(2)}, u32[]{:S(2)}) %all-to-all-start.1) | async-done | bytes 819232 | tf_op jit(solution)/shard_map/all_to_all | solution.py:247
  598.6 51.1 %all-gather.8.cloned.1.call-done = bf16[4096,3200]{1,0:T(8,128)(2,1)} async-done(((bf16[128,3200]{1,0:T(8,128)(2,1)}), bf16[4096,3200]{1,0:T(8,128)(2,1)}) %all-gather.8.cloned.1.call-update) | async-done | bytes 26214416 | tf_op jit(solution)/shard_map/all_gather | solution.py:45
  649.8 9.1 %fusion.378 = f32[100,1600]{1,0:T(8,128)S(1)} fusion(bf16[100,4096]{1,0:T(8,128)(2,1)S(1)} %bitcast.670, bf16[4096,3200]{1,0:T(8,128)(2,1)} %all-gather.8.cloned.1.call-done), kind=kOutput, calls=%fused_computation.573 | convolution fusion | flops 1310720000 | bytes 15090688 | tf_op jit(solution)/shard_map/dot_general | solution.py:252
  658.9 7.3 fusion.390
  667.0 12.1 %fusion.393 = f32[5,5]{1,0:T(8,128)S(1)} fusion(f32[1,1,100,1600]{3,0,2,1:T(1,128)S(1)} %copy.242, f32[1,1,100,1600]{3,0,2,1:T(1,128)S(1)} %bitcast.667, f32[1,1,100,1600]{3,0,2,1:T(1,128)S(1)} %bitcast.672, f32[2,1,100,1600]{3,0,2,1:T(2,128)S(1)} %copy-done.59), kind=kOutput, calls=%fused_computation.589 | convolution fusion | flops 50400000 | bytes 3200100 | tf_op jit(solution)/shard_map/dot_general | solution.py:257
  679.0 9.0 %psum.28 = f32[5,5]{1,0:T(8,128)S(1)} all-reduce(f32[5,5]{1,0:T(8,128)S(1)} %fusion.393), channel_id=1, replica_groups=mesh['section'=4,'dp_0'=4,'dp_1'=4,'dp_2'=2] {'section'}, use_global_device_ids=true, to_apply=%region_69.70 | all-reduce | flops 25 | bytes 200 | tf_op jit(solution)/shard_map/psum | solution.py:49
  688.0 8.4 %psum.29 = f32[5,5]{1,0:T(8,128)S(1)} all-reduce(f32[5,5]{1,0:T(8,128)S(1)} %psum.28), channel_id=1, replica_groups=mesh['section'=4,'dp_0'=4,'dp_1'=4,'dp_2'=2] {'dp_0'}, use_global_device_ids=true, to_apply=%region_70.71 | all-reduce | flops 25 | bytes 200 | tf_op jit(solution)/shard_map/psum | solution.py:49
  696.4 6.6 psum.30
  703.0 8.4 %psum.31 = f32[5,5]{1,0:T(8,128)S(1)} all-reduce(f32[5,5]{1,0:T(8,128)S(1)} %psum.30), channel_id=1, replica_groups=mesh['section'=4,'dp_0'=4,'dp_1'=4,'dp_2'=2] {'dp_2'}, use_global_device_ids=true, to_apply=%region_72.73 | all-reduce | flops 25 | bytes 200 | tf_op jit(solution)/shard_map/psum | solution.py:49
  (320 shorter events, 212.0 us)
Async XLA Ops:
  7.2 64.4 %all-gather.4.cloned.1.call-start = ((), (), s32[]{:S(2)}) async-start(), calls=%async_computation.2 | async-start | bytes 5883904 | tf_op jit(solution)/shard_map/all_gather | solution.py:22
  9.1 93.9 %all-gather.6.cloned.1.call-start = ((), (), s32[]{:S(2)}) async-start(), calls=%async_computation.3 | async-start | bytes 15974400 | tf_op jit(solution)/shard_map/all_gather | solution.py:22
  77.2 572.6 %all-gather.8.cloned.1.call-start = ((), (), s32[]{:S(2)}) async-start(), calls=%async_computation.4 | async-start | bytes 27033600 | tf_op jit(solution)/shard_map/all_gather | solution.py:45
  78.4 18.0 %copy-start.32 = (bf16[128,1600]{1,0:T(8,128)(2,1)}, bf16[128,1600]{1,0:T(8,128)(2,1)S(1)}, u32[]{:S(2)}) copy-start(bf16[128,1600]{1,0:T(8,128)(2,1)S(1)} %copy.177) | copy-start | bytes 1228804
  113.0 14.8 %copy-start.64 = (f32[1,1600]{1,0:T(1,128)S(1)}, f32[1,1600]{1,0:T(1,128)}, u32[]{:S(2)}) copy-start(f32[1,1600]{1,0:T(1,128)} %param.32) | copy-start | bytes 19204
  113.0 14.8 %copy-start.67 = (f32[1,3200]{1,0:T(1,128)S(1)}, f32[1,3200]{1,0:T(1,128)}, u32[]{:S(2)}) copy-start(f32[1,3200]{1,0:T(1,128)} %param.31) | copy-start | bytes 38404
  129.2 9.2 %slice-start.12 = ((s8[10649600]{0:T(1024)(128)(4,1)}), s8[4194304]{0:T(1024)(128)(4,1)S(1)}, s32[]{:S(2)}) async-start(s8[10649600]{0:T(1024)(128)(4,1)} %bitcast.634), calls=%async_computation.17 | async-start | bytes 8388608 | tf_op jit(solution)/shard_map/cond
  153.4 6.0 collective-permute-start
  154.8 9.1 %collective-permute-start.1 = (bf16[64,1600]{1,0:T(8,128)(2,1)S(1)}, bf16[64,1600]{1,0:T(8,128)(2,1)S(1)}, u32[]{:S(2)}, u32[]{:S(2)}) collective-permute-start(bf16[64,1600]{1,0:T(8,128)(2,1)S(1)} %get-tuple-element.919), channel_id=1, source_target_pairs={{0,32},{32,64},{64,96},{1,33},{33,65},{65,97},{2,34},{34,66},{66,9... | collective-permute-start | bytes 614408 | tf_op jit(solution)/shard_map/ppermute | solution.py:36
  169.9 9.5 %slice-start.15 = ((s8[10649600]{0:T(1024)(128)(4,1)}), s8[4194304]{0:T(1024)(128)(4,1)S(1)}, s32[]{:S(2)}) async-start(s8[10649600]{0:T(1024)(128)(4,1)} %bitcast.636), calls=%async_computation.20 | async-start | bytes 8388608 | tf_op jit(solution)/shard_map/cond
  201.1 10.1 %collective-permute-start.3 = (bf16[64,1600]{1,0:T(8,128)(2,1)}, bf16[64,1600]{1,0:T(8,128)(2,1)S(1)}, u32[]{:S(2)}, u32[]{:S(2)}) collective-permute-start(bf16[64,1600]{1,0:T(8,128)(2,1)} %copy.189), channel_id=1, source_target_pairs={{0,32},{32,64},{64,96},{1,33},{33,65},{65,97},{2,34},{34,66},{66,9... | collective-permute-start | bytes 614408 | tf_op jit(solution)/shard_map/ppermute | solution.py:36
  205.4 8.6 %collective-permute-start.2 = (bf16[64,1600]{1,0:T(8,128)(2,1)S(1)}, bf16[64,1600]{1,0:T(8,128)(2,1)S(1)}, u32[]{:S(2)}, u32[]{:S(2)}) collective-permute-start(bf16[64,1600]{1,0:T(8,128)(2,1)S(1)} %copy.188), channel_id=1, source_target_pairs={{0,32},{32,64},{64,96},{1,33},{33,65},{65,97},{2,34},{34,66},{66,9... | collective-permute-start | bytes 614408 | tf_op jit(solution)/shard_map/ppermute | solution.py:36
  224.0 38.9 %collective-permute-start.5 = (bf16[64,1600]{1,0:T(8,128)(2,1)}, bf16[64,1600]{1,0:T(8,128)(2,1)S(1)}, u32[]{:S(2)}, u32[]{:S(2)}) collective-permute-start(bf16[64,1600]{1,0:T(8,128)(2,1)} %copy.193), channel_id=1, source_target_pairs={{0,32},{32,64},{64,96},{1,33},{33,65},{65,97},{2,34},{34,66},{66,9... | collective-permute-start | bytes 614408 | tf_op jit(solution)/shard_map/ppermute | solution.py:36
  258.1 7.8 %collective-permute-start.4 = (bf16[64,1600]{1,0:T(8,128)(2,1)}, bf16[64,1600]{1,0:T(8,128)(2,1)S(1)}, u32[]{:S(2)}, u32[]{:S(2)}) collective-permute-start(bf16[64,1600]{1,0:T(8,128)(2,1)} %copy.192), channel_id=1, source_target_pairs={{0,32},{32,64},{64,96},{1,33},{33,65},{65,97},{2,34},{34,66},{66,9... | collective-permute-start | bytes 614408 | tf_op jit(solution)/shard_map/ppermute | solution.py:36
  275.7 39.0 %collective-permute-start.7 = (bf16[64,1600]{1,0:T(8,128)(2,1)}, bf16[64,1600]{1,0:T(8,128)(2,1)S(1)}, u32[]{:S(2)}, u32[]{:S(2)}) collective-permute-start(bf16[64,1600]{1,0:T(8,128)(2,1)} %copy.197), channel_id=1, source_target_pairs={{0,32},{32,64},{64,96},{1,33},{33,65},{65,97},{2,34},{34,66},{66,9... | collective-permute-start | bytes 614408 | tf_op jit(solution)/shard_map/ppermute | solution.py:36
  279.8 35.8 %collective-permute-start.6 = (bf16[64,1600]{1,0:T(8,128)(2,1)}, bf16[64,1600]{1,0:T(8,128)(2,1)S(1)}, u32[]{:S(2)}, u32[]{:S(2)}) collective-permute-start(bf16[64,1600]{1,0:T(8,128)(2,1)} %copy.196), channel_id=1, source_target_pairs={{0,32},{32,64},{64,96},{1,33},{33,65},{65,97},{2,34},{34,66},{66,9... | collective-permute-start | bytes 614408 | tf_op jit(solution)/shard_map/ppermute | solution.py:36
  326.2 13.3 %copy-start.16 = (bf16[2,64,1600]{2,1,0:T(8,128)(2,1)S(1)}, bf16[2,64,1600]{2,1,0:T(8,128)(2,1)}, u32[]{:S(2)}) copy-start(bf16[2,64,1600]{2,1,0:T(8,128)(2,1)} %copy-done.15) | copy-start | bytes 1228804
  328.7 7.1 collective-permute-start.9
  330.0 9.5 %collective-permute-start.8 = (bf16[64,1600]{1,0:T(8,128)(2,1)S(1)}, bf16[64,1600]{1,0:T(8,128)(2,1)S(1)}, u32[]{:S(2)}, u32[]{:S(2)}) collective-permute-start(bf16[64,1600]{1,0:T(8,128)(2,1)S(1)} %copy.219), channel_id=1, source_target_pairs={{32,0},{64,32},{96,64},{33,1},{65,33},{97,65},{34,2},{66,34},{98,6... | collective-permute-start | bytes 614408 | tf_op jit(solution)/shard_map/ppermute | solution.py:36
  344.3 7.4 %collective-permute-start.11 = (bf16[64,1600]{1,0:T(8,128)(2,1)S(1)}, bf16[64,1600]{1,0:T(8,128)(2,1)S(1)}, u32[]{:S(2)}, u32[]{:S(2)}) collective-permute-start(bf16[64,1600]{1,0:T(8,128)(2,1)S(1)} %copy.226), channel_id=1, source_target_pairs={{32,0},{64,32},{96,64},{33,1},{65,33},{97,65},{34,2},{66,34},{98,6... | collective-permute-start | bytes 614408 | tf_op jit(solution)/shard_map/ppermute | solution.py:36
  346.8 9.9 %collective-permute-start.10 = (bf16[64,1600]{1,0:T(8,128)(2,1)S(1)}, bf16[64,1600]{1,0:T(8,128)(2,1)S(1)}, u32[]{:S(2)}, u32[]{:S(2)}) collective-permute-start(bf16[64,1600]{1,0:T(8,128)(2,1)S(1)} %copy.225), channel_id=1, source_target_pairs={{32,0},{64,32},{96,64},{33,1},{65,33},{97,65},{34,2},{66,34},{98,6... | collective-permute-start | bytes 614408 | tf_op jit(solution)/shard_map/ppermute | solution.py:36
  361.5 124.2 %collective-permute-start.13 = (bf16[64,1600]{1,0:T(8,128)(2,1)S(1)}, bf16[64,1600]{1,0:T(8,128)(2,1)S(1)}, u32[]{:S(2)}, u32[]{:S(2)}) collective-permute-start(bf16[64,1600]{1,0:T(8,128)(2,1)S(1)} %copy.232), channel_id=1, source_target_pairs={{32,0},{64,32},{96,64},{33,1},{65,33},{97,65},{34,2},{66,34},{98,6... | collective-permute-start | bytes 614408 | tf_op jit(solution)/shard_map/ppermute | solution.py:36
  364.0 127.3 %collective-permute-start.12 = (bf16[64,1600]{1,0:T(8,128)(2,1)S(1)}, bf16[64,1600]{1,0:T(8,128)(2,1)S(1)}, u32[]{:S(2)}, u32[]{:S(2)}) collective-permute-start(bf16[64,1600]{1,0:T(8,128)(2,1)S(1)} %copy.231), channel_id=1, source_target_pairs={{32,0},{64,32},{96,64},{33,1},{65,33},{97,65},{34,2},{66,34},{98,6... | collective-permute-start | bytes 614408 | tf_op jit(solution)/shard_map/ppermute | solution.py:36
  493.2 34.9 %copy-start.1 = (bf16[2,64,1600]{2,1,0:T(8,128)(2,1)S(1)}, bf16[2,64,1600]{2,1,0:T(8,128)(2,1)}, u32[]{:S(2)}) copy-start(bf16[2,64,1600]{2,1,0:T(8,128)(2,1)} %copy-done) | copy-start | bytes 1228804
  495.6 15.7 %slice-start.9 = ((s8[10240000]{0:T(1024)(128)(4,1)}), s8[4194304]{0:T(1024)(128)(4,1)S(1)}, s32[]{:S(2)}) async-start(s8[10240000]{0:T(1024)(128)(4,1)} %bitcast.623), calls=%async_computation.14 | async-start | bytes 8388608 | tf_op jit(solution)/shard_map/cond
  495.6 15.7 %slice-start.10 = ((s8[10240000]{0:T(1024)(128)(4,1)}), s8[4194304]{0:T(1024)(128)(4,1)S(1)}, s32[]{:S(2)}) async-start(s8[10240000]{0:T(1024)(128)(4,1)} %bitcast.623), calls=%async_computation.15 | async-start | bytes 8388608 | tf_op jit(solution)/shard_map/cond
  521.5 6.6 collective-permute-start.15
  524.0 14.3 %copy-start.58 = (bf16[1,64,3200]{2,1,0:T(8,128)(2,1)S(1)}, bf16[1,64,3200]{2,1,0:T(8,128)(2,1)}, u32[]{:S(2)}) copy-start(bf16[1,64,3200]{2,1,0:T(8,128)(2,1)} %copy-done.57) | copy-start | bytes 1228804
  524.1 9.9 %collective-permute-start.14 = (bf16[64,1600]{1,0:T(8,128)(2,1)S(1)}, bf16[64,1600]{1,0:T(8,128)(2,1)S(1)}, u32[]{:S(2)}, u32[]{:S(2)}) collective-permute-start(bf16[64,1600]{1,0:T(8,128)(2,1)S(1)} %copy.237), channel_id=1, source_target_pairs={{32,0},{64,32},{96,64},{33,1},{65,33},{97,65},{34,2},{66,34},{98,6... | collective-permute-start | bytes 614408 | tf_op jit(solution)/shard_map/ppermute | solution.py:36
  542.5 32.6 %all-to-all-start = ((bf16[32,100,128]{2,1,0:T(8,128)(2,1)}), bf16[32,100,128]{2,1,0:T(8,128)(2,1)}, u32[]{:S(2)}, u32[]{:S(2)}) async-start(bf16[32,100,128]{2,1,0:T(8,128)(2,1)} %all_to_all.28), calls=%async_computation | async-start | bytes 1703936 | tf_op jit(solution)/shard_map/all_to_all | solution.py:248
  552.5 28.8 %copy-start.30 = (f32[2,1,100,1600]{3,1,2,0:T(1,128)S(1)}, f32[2,1,100,1600]{3,1,2,0:T(1,128)}, u32[]{:S(2)}) copy-start(f32[2,1,100,1600]{3,1,2,0:T(1,128)} %param.36) | copy-start | bytes 3840004
  575.1 23.0 %all-to-all-start.1 = ((bf16[32,100,128]{2,1,0:T(8,128)(2,1)}), bf16[32,100,128]{2,1,0:T(8,128)(2,1)S(1)}, u32[]{:S(2)}, u32[]{:S(2)}) async-start(bf16[32,100,128]{2,1,0:T(8,128)(2,1)} %all_to_all.32), calls=%async_computation.1 | async-start | bytes 1703936 | tf_op jit(solution)/shard_map/all_to_all | solution.py:247
  (37 other events, 174.3 us)
Sparse Core Ops, SparseCore 0:
  10.7 60.7 all-gather.3
  77.3 25.6 all-gather.5
  538.4 111.3 all-gather.7
where the time goes:
time: 739 us; the launch traced here: 732 us
  waiting for transfers between devices  306 us (41%)
  local copies, waits for them, and re-layouts  113 us (15%)
  starting transfers between devices  108 us (15%)
  matrix products  85.4 us (12%)
  other arithmetic  66.4 us (9%)
  blocking collectives  32.3 us (4%)
  between operations  19 us (3%)
    ppermute x16, waiting for transfers between devices, from_behind(): lax.ppermute(value, axis, [(source, source + steps) for source in range(i...  153 us
    ppermute x16, starting transfers between devices, from_behind(): lax.ppermute(value, axis, [(source, source + steps) for source in range(i...  92.7 us
    all_gather x2, waiting for transfers between devices, gather_in_order(): blocks = lax.all_gather(blocks, axes[k], axis=0, tiled=True)  68.9 us
    all_gather x1, waiting for transfers between devices, sent_together(): lax.all_gather(both, axis, axis=dim, tiled=True)  51.1 us
    select_n x46, other arithmetic, store_block(): jnp.where(active, lax.dynamic_update_index_in_dim(stack, block, position,...  36.1 us
    psum x4, blocking collectives, over_axes(): return functools.reduce(lax.psum, axes, value)  32.3 us
    unnamed x76, local copies, waits for them, and re-layouts  26.7 us
    all_to_all x1, waiting for transfers between devices, body(): lax.all_to_all(hidden_dot_rows.T, DP, split_axis=0, concat_axis=1, tiled=...  20.7 us
  transfers between devices with their start and end apart: 21, of which 17 were waited for; matrix products, arithmetic and copies ran while one was open for 7% of the time, Pallas kernels for 0%

commit v1 on v0

--- a/solution.py
+++ b/solution.py
@@ -19,7 +19,10 @@
 def gather_in_order(value, axes, turns):
     blocks = value[None]
     for k in turns:
-        blocks = lax.all_gather(blocks, axes[k], axis=0, tiled=True)
+        size = lax.axis_size(axes[k])
+        parts = jnp.stack([blocks for _ in range(size)])
+        parts = lax.all_to_all(parts, axes[k], split_axis=0, concat_axis=0)
+        blocks = jnp.concatenate(parts, axis=0)
     carried = [lax.axis_size(axes[k]) for k in reversed(turns)]
     blocks = blocks.reshape(*carried, *value.shape)
     turned = sorted(range(len(turns)), key=lambda place: turns[len(turns) - 1 - place])

time: 739 us -> 769 us (1.041)
  blocking collectives: 32.3 us -> 46.7 us
  starting transfers between devices: 108 us -> 121 us
  other arithmetic: 66.4 us -> 75.8 us
    all_gather x2 -> x0, waiting for transfers between devices: 68.9 us -> none  [gather_in_order(): blocks = lax.all_gather(blocks, axes[k], axis=0, tiled=True)]
    all_to_all x0 -> x1, waiting for transfers between devices: none -> 67.7 us  [gather_in_order(): parts = lax.all_to_all(parts, axes[k], split_axis=0, concat_axis=0)]
    all_to_all x0 -> x1, blocking collectives: none -> 14.3 us  [gather_in_order(): parts = lax.all_to_all(parts, axes[k], split_axis=0, concat_axis=0)]
    reshape x1 -> x0, local copies, waits for them, and re-layouts: 10 us -> none  [gather_in_order(): blocks = blocks.reshape(*carried, *value.shape)]
    all_to_all x0 -> x1, starting transfers between devices: none -> 8.59 us  [gather_in_order(): parts = lax.all_to_all(parts, axes[k], split_axis=0, concat_axis=0)]
    another operation x5 -> x6, other arithmetic: 0.15 us -> 8 us  [the longest x1 7.85 us: gather_in_order(): parts = jnp.stack([blocks for _ in range(size)])]
  transfers between devices with their start and end apart: 21 -> 20, of which waited for: 17 -> 16; matrix products, arithmetic and copies ran while one was open for 7% -> 7% of each run, Pallas kernels for 0% -> 0%
where the time goes in v1:
time: 769 us; the launch traced here: 761 us
  waiting for transfers between devices  304 us (40%)
  starting transfers between devices  121 us (16%)
  local copies, waits for them, and re-layouts  107 us (14%)
  matrix products  85.4 us (11%)
  other arithmetic  75.8 us (10%)
  blocking collectives  46.7 us (6%)
  between operations  19.4 us (3%)
    ppermute x16, waiting for transfers between devices, from_behind(): lax.ppermute(value, axis, [(source, source + steps) for source in range(i...  152 us
    ppermute x16, starting transfers between devices, from_behind(): lax.ppermute(value, axis, [(source, source + steps) for source in range(i...  92.8 us
    all_to_all x1, waiting for transfers between devices, gather_in_order(): parts = lax.all_to_all(parts, axes[k], split_axis=0, concat_axis=0)  67.7 us
    all_gather x1, waiting for transfers between devices, sent_together(): lax.all_gather(both, axis, axis=dim, tiled=True)  51.4 us
    select_n x46, other arithmetic, store_block(): jnp.where(active, lax.dynamic_update_index_in_dim(stack, block, position,...  36 us
    psum x4, blocking collectives, over_axes(): return functools.reduce(lax.psum, axes, value)  32.3 us
    unnamed x76, local copies, waits for them, and re-layouts  23.4 us
    all_to_all x1, waiting for transfers between devices, body(): lax.all_to_all(hidden_dot_rows.T, DP, split_axis=0, concat_axis=1, tiled=...  20.7 us
  transfers between devices with their start and end apart: 20, of which 16 were waited for; matrix products, arithmetic and copies ran while one was open for 7% of the time, Pallas kernels for 0%

profile of v1, /device:TPU:1, one launch (start us, length us, event | category | flops | bytes accessed | tf_op | source)
XLA Modules:
  0.0 761.5 jit_solution(4907670609314963355)
XLA Ops:
  11.6 8.6 %all-to-all-start = ((bf16[16,1,100,1600]{3,2,1,0:T(8,128)(2,1)}), bf16[16,1,100,1600]{3,2,1,0:T(8,128)(2,1)}, u32[]{:S(2)}, u32[]{:S(2)}) async-start(bf16[16,1,100,1600]{3,2,1,0:T(8,128)(2,1)} %stack.15), calls=%async_computation | async-start | bytes 11075584 | tf_op jit(solution)/shard_map/all_to_all | solution.py:24
  21.6 16.2 %copy.102 = bf16[1,3200,1600]{2,1,0:T(8,128)(2,1)} copy(bf16[1,3200,1600]{1,2,0:T(8,128)(2,1)} %param.33) | data formatting | bytes 20480000 | tf_op args[5]
  38.0 67.7 %all-to-all-done = bf16[16,1,100,1600]{3,2,1,0:T(8,128)(2,1)} async-done(((bf16[16,1,100,1600]{3,2,1,0:T(8,128)(2,1)}), bf16[16,1,100,1600]{3,2,1,0:T(8,128)(2,1)}, u32[]{:S(2)}, u32[]{:S(2)}) %all-to-all-start) | async-done | bytes 5120032 | tf_op jit(solution)/shard_map/all_to_all | solution.py:24
  105.7 7.8 %pad_maximum_fusion = bf16[2,16,100,1600]{3,2,1,0:T(8,128)(2,1)S(1)} fusion(bf16[1,16,100,1600]{3,2,1,0:T(8,128)(2,1)} %bitcast.48), kind=kLoop, calls=%fused_computation.577 | loop fusion | flops 5120000 | bytes 15360000 | tf_op jit(solution)/shard_map/stack | solution.py:23
  117.5 14.3 %all_to_all.48 = bf16[2,16,100,1600]{3,1,2,0:T(8,128)(2,1)S(1)} all-to-all(bf16[2,16,100,1600]{3,1,2,0:T(8,128)(2,1)S(1)} %copy.103), channel_id=1, replica_groups=mesh['section'=4,'dp_0'=4,'dp_1'=4,'dp_2'=2] {'dp_2'}, dimensions={0} | all-to-all | bytes 20480000 | tf_op jit(solution)/shard_map/all_to_all | solution.py:24
  131.8 6.5 copy.104
  138.3 14.7 %reshape_reshape.3 = bf16[3200,1600]{1,0:T(8,128)(2,1)} reshape(bf16[16,2,100,1600]{3,2,1,0:T(8,128)(2,1)} %copy.104) | data formatting | bytes 20480000 | tf_op jit(solution)/shard_map/reshape;reshape | solution.py:16
  153.0 25.5 %conditional.9 = (f32[64,3200]{1,0:T(8,128)}, f32[64,3200]{1,0:T(8,128)S(1)}, bf16[1,64,3200]{2,1,0:T(8,128)(2,1)S(1)}, bf16[1,64,3200]{2,1,0:T(8,128)(2,1)}, bf...) conditional(s32[]{:T(128)} %convert_element_type.473, () %tuple.151, (bf16[1,64,1600]{2,1,0:T(8,128)(2,1)S(1)}, ...), branch_computations={%region_0.1_spmd, %region_1.5_spmd} | conditional | flops 3289190656 | bytes 78807200 | solution.py:170
  154.8 5.9 fusion.29
  168.0 8.2 %fusion = bf16[64,1600]{0,1:T(8,128)(2,1)S(1)} fusion(bf16[64,3200]{1,0:T(8,128)(2,1)S(1)} %multiply_convert_fusion, bf16[3200,1600]{1,0:T(8,128)(2,1)} %get-tuple-element.500, f32[128,1600]{0,1:T(8,128)S(1)} %fusion.25), kind=kOutput, calls=%fused_computation.1 | convolution fusion | flops 655564800 | bytes 11264000 | tf_op jit(solution)/shard_map/cond/branch_1_fun/dot_general | solution.py:151
  189.0 34.2 %conditional.10 = (bf16[64,1600]{0,1:T(8,128)(2,1)}, bf16[64,1600]{0,1:T(8,128)(2,1)}, f32[1,64,3200]{2,1,0:T(8,128)}, f32[1,64,3200]{2,1,0:T(8,128)}, bf16[1,64...) conditional(s32[]{:T(128)} %convert_element_type.476, ...), branch_computations={%region_5.6_spmd, %region_6.11_spmd} | conditional | flops 3286835456 | bytes 77476808 | solution.py:170
  196.6 5.9 fusion.68
  210.0 9.1 %fusion.36 = bf16[64,1600]{0,1:T(8,128)(2,1)} fusion(bf16[64,3200]{1,0:T(8,128)(2,1)} %get-tuple-element.927, bf16[3200,1600]{1,0:T(8,128)(2,1)} %get-tuple-element.507, bf16[64,1600]{0,1:T(8,128)(2,1)S(1)} %copy-done.21, f32[128,1600]{0,1:T(8,128)S(1)} %fusion.63), kind=kOutput, calls=%fused_computation.50 | convolution fusion | flops 655769600 | bytes 11468800 | tf_op jit(solution)/shard_map/cond/branch_1_fun/dot_general | solution.py:151
  239.8 5.5 conditional.11
  249.0 34.1 %collective-permute-start.5 = (bf16[64,1600]{1,0:T(8,128)(2,1)}, bf16[64,1600]{1,0:T(8,128)(2,1)S(1)}, u32[]{:S(2)}, u32[]{:S(2)}) collective-permute-start(bf16[64,1600]{1,0:T(8,128)(2,1)} %copy.116), channel_id=1, source_target_pairs={{0,32},{32,64},{64,96},{1,33},{33,65},{65,97},{2,34},{34,66},{66,9... | collective-permute-start | bytes 614408 | tf_op jit(solution)/shard_map/ppermute | solution.py:39
  304.8 32.4 %collective-permute-start.6 = (bf16[64,1600]{1,0:T(8,128)(2,1)}, bf16[64,1600]{1,0:T(8,128)(2,1)S(1)}, u32[]{:S(2)}, u32[]{:S(2)}) collective-permute-start(bf16[64,1600]{1,0:T(8,128)(2,1)} %copy.119), channel_id=1, source_target_pairs={{0,32},{32,64},{64,96},{1,33},{33,65},{65,97},{2,34},{34,66},{66,9... | collective-permute-start | bytes 614408 | tf_op jit(solution)/shard_map/ppermute | solution.py:39
  390.1 120.3 %collective-permute-done.13 = bf16[64,1600]{1,0:T(8,128)(2,1)S(1)} collective-permute-done((bf16[64,1600]{1,0:T(8,128)(2,1)S(1)}, bf16[64,1600]{1,0:T(8,128)(2,1)S(1)}, u32[]{:S(2)}, u32[]{:S(2)}) %collective-permute-start.13) | collective-permute-done | bytes 204832 | tf_op jit(solution)/shard_map/ppermute | solution.py:39
  517.7 27.2 %conditional.17 = (bf16[64,1600]{0,1:T(8,128)(2,1)}, bf16[64,1600]{0,1:T(8,128)(2,1)}) conditional(s32[]{:T(128)} %convert_element_type.512, () %tuple.167, (bf16[64,1600]{1,0:T(8,128)(2,1)S(1)}, f32[2,64,3200]{2,1,0:T(8,128)S(1)}, s32[]{:T(128)}, bf16[64,1600]{1,0:T(8,128)(2,1)S(1)}, bf16[3200,1600]{1,0:T(8,128)(2,1)}, ...), branch_computations={%region_59.60_spmd, %region_60.69_spmd} | conditional | flops 3295233024 | bytes 87697088 | solution.py:240
  520.2 7.7 %fusion.369 = f32[128,3200]{1,0:T(8,128)S(1)} fusion(bf16[3200,1600]{1,0:T(8,128)(2,1)} %get-tuple-element.568, bf16[64,1600]{0,1:T(8,128)(2,1)S(1)} %copy.157, bf16[64,1600]{0,1:T(8,128)(2,1)} %copy.156), kind=kOutput, calls=%fused_computation.554 | convolution fusion | flops 1311539200 | bytes 12288000 | tf_op jit(solution)/shard_map/cond/branch_1_fun/dot_general | solution.py:75
  527.9 7.4 fusion.334
  567.0 14.4 %all-to-all-start.2 = ((bf16[32,100,128]{2,1,0:T(8,128)(2,1)}), bf16[32,100,128]{2,1,0:T(8,128)(2,1)}, u32[]{:S(2)}, u32[]{:S(2)}) async-start(bf16[32,100,128]{2,1,0:T(8,128)(2,1)} %all_to_all.36), calls=%async_computation.2 | async-start | bytes 1703936 | tf_op jit(solution)/shard_map/all_to_all | solution.py:251
  583.4 20.7 %all-to-all-done.2 = bf16[32,100,128]{2,1,0:T(8,128)(2,1)} async-done(((bf16[32,100,128]{2,1,0:T(8,128)(2,1)}), bf16[32,100,128]{2,1,0:T(8,128)(2,1)}, u32[]{:S(2)}, u32[]{:S(2)}) %all-to-all-start.2) | async-done | bytes 819232 | tf_op jit(solution)/shard_map/all_to_all | solution.py:251
  604.0 5.5 all-to-all-start.3
  614.6 12.2 %all-to-all-done.3 = bf16[32,100,128]{2,1,0:T(8,128)(2,1)S(1)} async-done(((bf16[32,100,128]{2,1,0:T(8,128)(2,1)}), bf16[32,100,128]{2,1,0:T(8,128)(2,1)S(1)}, u32[]{:S(2)}, u32[]{:S(2)}) %all-to-all-start.3) | async-done | bytes 819232 | tf_op jit(solution)/shard_map/all_to_all | solution.py:250
  627.4 51.4 %all-gather.2.cloned.1.call-done = bf16[4096,3200]{1,0:T(8,128)(2,1)} async-done(((bf16[128,3200]{1,0:T(8,128)(2,1)}), bf16[4096,3200]{1,0:T(8,128)(2,1)}) %all-gather.2.cloned.1.call-update) | async-done | bytes 26214416 | tf_op jit(solution)/shard_map/all_gather | solution.py:48
  678.7 9.1 %fusion.378 = f32[100,1600]{1,0:T(8,128)S(1)} fusion(bf16[100,4096]{1,0:T(8,128)(2,1)S(1)} %bitcast.671, bf16[4096,3200]{1,0:T(8,128)(2,1)} %all-gather.2.cloned.1.call-done), kind=kOutput, calls=%fused_computation.573 | convolution fusion | flops 1310720000 | bytes 15090688 | tf_op jit(solution)/shard_map/dot_general | solution.py:255
  687.9 7.3 fusion.390
  695.9 12.1 %fusion.393 = f32[5,5]{1,0:T(8,128)S(1)} fusion(f32[1,1,100,1600]{3,0,2,1:T(1,128)S(1)} %copy.165, f32[1,1,100,1600]{3,0,2,1:T(1,128)S(1)} %bitcast.667, f32[1,1,100,1600]{3,0,2,1:T(1,128)S(1)} %bitcast.673, f32[2,1,100,1600]{3,0,2,1:T(2,128)S(1)} %copy-done.59), kind=kOutput, calls=%fused_computation.589 | convolution fusion | flops 50400000 | bytes 3200100 | tf_op jit(solution)/shard_map/dot_general | solution.py:260
  708.0 9.0 %psum.28 = f32[5,5]{1,0:T(8,128)S(1)} all-reduce(f32[5,5]{1,0:T(8,128)S(1)} %fusion.393), channel_id=1, replica_groups=mesh['section'=4,'dp_0'=4,'dp_1'=4,'dp_2'=2] {'section'}, use_global_device_ids=true, to_apply=%region_69.70 | all-reduce | flops 25 | bytes 200 | tf_op jit(solution)/shard_map/psum | solution.py:52
  717.0 8.4 %psum.29 = f32[5,5]{1,0:T(8,128)S(1)} all-reduce(f32[5,5]{1,0:T(8,128)S(1)} %psum.28), channel_id=1, replica_groups=mesh['section'=4,'dp_0'=4,'dp_1'=4,'dp_2'=2] {'dp_0'}, use_global_device_ids=true, to_apply=%region_70.71 | all-reduce | flops 25 | bytes 200 | tf_op jit(solution)/shard_map/psum | solution.py:52
  725.4 6.5 psum.30
  731.9 8.4 %psum.31 = f32[5,5]{1,0:T(8,128)S(1)} all-reduce(f32[5,5]{1,0:T(8,128)S(1)} %psum.30), channel_id=1, replica_groups=mesh['section'=4,'dp_0'=4,'dp_1'=4,'dp_2'=2] {'dp_2'}, use_global_device_ids=true, to_apply=%region_72.73 | all-reduce | flops 25 | bytes 200 | tf_op jit(solution)/shard_map/psum | solution.py:52
  (320 shorter events, 222.2 us)
Async XLA Ops:
  11.6 94.1 %all-to-all-start = ((bf16[16,1,100,1600]{3,2,1,0:T(8,128)(2,1)}), bf16[16,1,100,1600]{3,2,1,0:T(8,128)(2,1)}, u32[]{:S(2)}, u32[]{:S(2)}) async-start(bf16[16,1,100,1600]{3,2,1,0:T(8,128)(2,1)} %stack.15), calls=%async_computation | async-start | bytes 11075584 | tf_op jit(solution)/shard_map/all_to_all | solution.py:24
  20.2 658.5 %all-gather.2.cloned.1.call-start = ((), (), s32[]{:S(2)}) async-start(), calls=%async_computation.4 | async-start | bytes 27033600 | tf_op jit(solution)/shard_map/all_gather | solution.py:48
  20.6 17.3 %copy-start.32 = (bf16[128,1600]{1,0:T(8,128)(2,1)}, bf16[128,1600]{1,0:T(8,128)(2,1)S(1)}, u32[]{:S(2)}) copy-start(bf16[128,1600]{1,0:T(8,128)(2,1)S(1)} %copy.101) | copy-start | bytes 1228804
  138.3 14.7 %copy-start.64 = (f32[1,1600]{1,0:T(1,128)S(1)}, f32[1,1600]{1,0:T(1,128)}, u32[]{:S(2)}) copy-start(f32[1,1600]{1,0:T(1,128)} %param.32) | copy-start | bytes 19204
  138.3 14.7 %copy-start.67 = (f32[1,3200]{1,0:T(1,128)S(1)}, f32[1,3200]{1,0:T(1,128)}, u32[]{:S(2)}) copy-start(f32[1,3200]{1,0:T(1,128)} %param.31) | copy-start | bytes 38404
  154.5 9.2 %slice-start.12 = ((s8[10649600]{0:T(1024)(128)(4,1)}), s8[4194304]{0:T(1024)(128)(4,1)S(1)}, s32[]{:S(2)}) async-start(s8[10649600]{0:T(1024)(128)(4,1)} %bitcast.635), calls=%async_computation.17 | async-start | bytes 8388608 | tf_op jit(solution)/shard_map/cond
  178.6 5.8 collective-permute-start
  180.0 8.9 %collective-permute-start.1 = (bf16[64,1600]{1,0:T(8,128)(2,1)S(1)}, bf16[64,1600]{1,0:T(8,128)(2,1)S(1)}, u32[]{:S(2)}, u32[]{:S(2)}) collective-permute-start(bf16[64,1600]{1,0:T(8,128)(2,1)S(1)} %get-tuple-element.836), channel_id=1, source_target_pairs={{0,32},{32,64},{64,96},{1,33},{33,65},{65,97},{2,34},{34,66},{66,9... | collective-permute-start | bytes 614408 | tf_op jit(solution)/shard_map/ppermute | solution.py:39
  195.0 9.5 %slice-start.15 = ((s8[10649600]{0:T(1024)(128)(4,1)}), s8[4194304]{0:T(1024)(128)(4,1)S(1)}, s32[]{:S(2)}) async-start(s8[10649600]{0:T(1024)(128)(4,1)} %bitcast.637), calls=%async_computation.20 | async-start | bytes 8388608 | tf_op jit(solution)/shard_map/cond
  210.0 9.2 %copy-start.17 = (bf16[64,1600]{0,1:T(8,128)(2,1)S(1)}, bf16[64,1600]{0,1:T(8,128)(2,1)}, u32[]{:S(2)}) copy-start(bf16[64,1600]{0,1:T(8,128)(2,1)} %copy.109) | copy-start | bytes 614404 | tf_op jit(solution)/shard_map/cond
  226.3 10.1 %collective-permute-start.3 = (bf16[64,1600]{1,0:T(8,128)(2,1)}, bf16[64,1600]{1,0:T(8,128)(2,1)S(1)}, u32[]{:S(2)}, u32[]{:S(2)}) collective-permute-start(bf16[64,1600]{1,0:T(8,128)(2,1)} %copy.112), channel_id=1, source_target_pairs={{0,32},{32,64},{64,96},{1,33},{33,65},{65,97},{2,34},{34,66},{66,9... | collective-permute-start | bytes 614408 | tf_op jit(solution)/shard_map/ppermute | solution.py:39
  230.5 8.4 %collective-permute-start.2 = (bf16[64,1600]{1,0:T(8,128)(2,1)S(1)}, bf16[64,1600]{1,0:T(8,128)(2,1)S(1)}, u32[]{:S(2)}, u32[]{:S(2)}) collective-permute-start(bf16[64,1600]{1,0:T(8,128)(2,1)S(1)} %copy.111), channel_id=1, source_target_pairs={{0,32},{32,64},{64,96},{1,33},{33,65},{65,97},{2,34},{34,66},{66,9... | collective-permute-start | bytes 614408 | tf_op jit(solution)/shard_map/ppermute | solution.py:39
  249.0 38.9 %collective-permute-start.5 = (bf16[64,1600]{1,0:T(8,128)(2,1)}, bf16[64,1600]{1,0:T(8,128)(2,1)S(1)}, u32[]{:S(2)}, u32[]{:S(2)}) collective-permute-start(bf16[64,1600]{1,0:T(8,128)(2,1)} %copy.116), channel_id=1, source_target_pairs={{0,32},{32,64},{64,96},{1,33},{33,65},{65,97},{2,34},{34,66},{66,9... | collective-permute-start | bytes 614408 | tf_op jit(solution)/shard_map/ppermute | solution.py:39
  283.2 7.7 %collective-permute-start.4 = (bf16[64,1600]{1,0:T(8,128)(2,1)}, bf16[64,1600]{1,0:T(8,128)(2,1)S(1)}, u32[]{:S(2)}, u32[]{:S(2)}) collective-permute-start(bf16[64,1600]{1,0:T(8,128)(2,1)} %copy.115), channel_id=1, source_target_pairs={{0,32},{32,64},{64,96},{1,33},{33,65},{65,97},{2,34},{34,66},{66,9... | collective-permute-start | bytes 614408 | tf_op jit(solution)/shard_map/ppermute | solution.py:39
  300.8 39.0 %collective-permute-start.7 = (bf16[64,1600]{1,0:T(8,128)(2,1)}, bf16[64,1600]{1,0:T(8,128)(2,1)S(1)}, u32[]{:S(2)}, u32[]{:S(2)}) collective-permute-start(bf16[64,1600]{1,0:T(8,128)(2,1)} %copy.120), channel_id=1, source_target_pairs={{0,32},{32,64},{64,96},{1,33},{33,65},{65,97},{2,34},{34,66},{66,9... | collective-permute-start | bytes 614408 | tf_op jit(solution)/shard_map/ppermute | solution.py:39
  304.8 35.8 %collective-permute-start.6 = (bf16[64,1600]{1,0:T(8,128)(2,1)}, bf16[64,1600]{1,0:T(8,128)(2,1)S(1)}, u32[]{:S(2)}, u32[]{:S(2)}) collective-permute-start(bf16[64,1600]{1,0:T(8,128)(2,1)} %copy.119), channel_id=1, source_target_pairs={{0,32},{32,64},{64,96},{1,33},{33,65},{65,97},{2,34},{34,66},{66,9... | collective-permute-start | bytes 614408 | tf_op jit(solution)/shard_map/ppermute | solution.py:39
  351.2 12.9 %copy-start.16 = (bf16[2,64,1600]{2,1,0:T(8,128)(2,1)S(1)}, bf16[2,64,1600]{2,1,0:T(8,128)(2,1)}, u32[]{:S(2)}) copy-start(bf16[2,64,1600]{2,1,0:T(8,128)(2,1)} %copy-done.15) | copy-start | bytes 1228804
  353.6 7.0 collective-permute-start.9
  354.9 9.1 %collective-permute-start.8 = (bf16[64,1600]{1,0:T(8,128)(2,1)S(1)}, bf16[64,1600]{1,0:T(8,128)(2,1)S(1)}, u32[]{:S(2)}, u32[]{:S(2)}) collective-permute-start(bf16[64,1600]{1,0:T(8,128)(2,1)S(1)} %copy.142), channel_id=1, source_target_pairs={{32,0},{64,32},{96,64},{33,1},{65,33},{97,65},{34,2},{66,34},{98,6... | collective-permute-start | bytes 614408 | tf_op jit(solution)/shard_map/ppermute | solution.py:39
  368.8 7.5 collective-permute-start.11
  371.3 9.9 %collective-permute-start.10 = (bf16[64,1600]{1,0:T(8,128)(2,1)S(1)}, bf16[64,1600]{1,0:T(8,128)(2,1)S(1)}, u32[]{:S(2)}, u32[]{:S(2)}) collective-permute-start(bf16[64,1600]{1,0:T(8,128)(2,1)S(1)} %copy.148), channel_id=1, source_target_pairs={{32,0},{64,32},{96,64},{33,1},{65,33},{97,65},{34,2},{66,34},{98,6... | collective-permute-start | bytes 614408 | tf_op jit(solution)/shard_map/ppermute | solution.py:39
  386.1 124.3 %collective-permute-start.13 = (bf16[64,1600]{1,0:T(8,128)(2,1)S(1)}, bf16[64,1600]{1,0:T(8,128)(2,1)S(1)}, u32[]{:S(2)}, u32[]{:S(2)}) collective-permute-start(bf16[64,1600]{1,0:T(8,128)(2,1)S(1)} %copy.155), channel_id=1, source_target_pairs={{32,0},{64,32},{96,64},{33,1},{65,33},{97,65},{34,2},{66,34},{98,6... | collective-permute-start | bytes 614408 | tf_op jit(solution)/shard_map/ppermute | solution.py:39
  388.6 127.2 %collective-permute-start.12 = (bf16[64,1600]{1,0:T(8,128)(2,1)S(1)}, bf16[64,1600]{1,0:T(8,128)(2,1)S(1)}, u32[]{:S(2)}, u32[]{:S(2)}) collective-permute-start(bf16[64,1600]{1,0:T(8,128)(2,1)S(1)} %copy.154), channel_id=1, source_target_pairs={{32,0},{64,32},{96,64},{33,1},{65,33},{97,65},{34,2},{66,34},{98,6... | collective-permute-start | bytes 614408 | tf_op jit(solution)/shard_map/ppermute | solution.py:39
  517.7 35.0 %copy-start.1 = (bf16[2,64,1600]{2,1,0:T(8,128)(2,1)S(1)}, bf16[2,64,1600]{2,1,0:T(8,128)(2,1)}, u32[]{:S(2)}) copy-start(bf16[2,64,1600]{2,1,0:T(8,128)(2,1)} %copy-done) | copy-start | bytes 1228804
  520.2 15.7 %slice-start.9 = ((s8[10240000]{0:T(1024)(128)(4,1)}), s8[4194304]{0:T(1024)(128)(4,1)S(1)}, s32[]{:S(2)}) async-start(s8[10240000]{0:T(1024)(128)(4,1)} %bitcast.624), calls=%async_computation.14 | async-start | bytes 8388608 | tf_op jit(solution)/shard_map/cond
  520.2 15.7 %slice-start.10 = ((s8[10240000]{0:T(1024)(128)(4,1)}), s8[4194304]{0:T(1024)(128)(4,1)S(1)}, s32[]{:S(2)}) async-start(s8[10240000]{0:T(1024)(128)(4,1)} %bitcast.624), calls=%async_computation.15 | async-start | bytes 8388608 | tf_op jit(solution)/shard_map/cond
  546.1 6.6 collective-permute-start.15
  548.6 14.2 %copy-start.58 = (bf16[1,64,3200]{2,1,0:T(8,128)(2,1)S(1)}, bf16[1,64,3200]{2,1,0:T(8,128)(2,1)}, u32[]{:S(2)}) copy-start(bf16[1,64,3200]{2,1,0:T(8,128)(2,1)} %copy-done.57) | copy-start | bytes 1228804
  548.6 9.8 %collective-permute-start.14 = (bf16[64,1600]{1,0:T(8,128)(2,1)S(1)}, bf16[64,1600]{1,0:T(8,128)(2,1)S(1)}, u32[]{:S(2)}, u32[]{:S(2)}) collective-permute-start(bf16[64,1600]{1,0:T(8,128)(2,1)S(1)} %copy.160), channel_id=1, source_target_pairs={{32,0},{64,32},{96,64},{33,1},{65,33},{97,65},{34,2},{66,34},{98,6... | collective-permute-start | bytes 614408 | tf_op jit(solution)/shard_map/ppermute | solution.py:39
  567.0 37.1 %all-to-all-start.2 = ((bf16[32,100,128]{2,1,0:T(8,128)(2,1)}), bf16[32,100,128]{2,1,0:T(8,128)(2,1)}, u32[]{:S(2)}, u32[]{:S(2)}) async-start(bf16[32,100,128]{2,1,0:T(8,128)(2,1)} %all_to_all.36), calls=%async_computation.2 | async-start | bytes 1703936 | tf_op jit(solution)/shard_map/all_to_all | solution.py:251
  581.5 28.7 %copy-start.30 = (f32[2,1,100,1600]{3,1,2,0:T(1,128)S(1)}, f32[2,1,100,1600]{3,1,2,0:T(1,128)}, u32[]{:S(2)}) copy-start(f32[2,1,100,1600]{3,1,2,0:T(1,128)} %param.36) | copy-start | bytes 3840004
  604.0 22.8 %all-to-all-start.3 = ((bf16[32,100,128]{2,1,0:T(8,128)(2,1)}), bf16[32,100,128]{2,1,0:T(8,128)(2,1)S(1)}, u32[]{:S(2)}, u32[]{:S(2)}) async-start(bf16[32,100,128]{2,1,0:T(8,128)(2,1)} %all_to_all.40), calls=%async_computation.3 | async-start | bytes 1703936 | tf_op jit(solution)/shard_map/all_to_all | solution.py:250
  (36 other events, 179.3 us)
Sparse Core Ops, SparseCore 0:
  562.8 115.8 all-gather.1
